TPU v7x, 32 devices: a whole 2x2x4 slice. The times are simulated.
32 devices in a mesh: group: 8 (over z, x), tensor: 4 (over y, core).
Axes of the slice: x: 2, y: 2, z: 4, core: 2. Of those that a mesh axis runs over, the one named last changes fastest.
Arguments:
- queries: bfloat16 [64, 64, 5120], P('group', None, 'tensor'), may hold values from -15 to 15
- prefix_keys: bfloat16 [16, 1024, 1024], P('group', None, 'tensor'), may hold values from -200 to 200
- prefix_values: bfloat16 [16, 1024, 1024], P('group', None, 'tensor'), may hold values from -6 to 6
- slot_of_prompt: int32 [16], replicated, may hold values from 0 to 15, as said below
- prompt_of: int32 [64], P('group'), may hold values from 0 to 15, as said below
- lengths: int32 [64], P('group'), may hold values from 1 to 64
Outputs:
- attended: bfloat16 [64, 64, 5120], P('group', 'tensor')
Inputs may be any that keep to these rules, and one draw needn't show every extreme that they name: A permutation: prompt p's keys and values lie in row slot_of_prompt[p] of the prefix arrays, and that row belongs to group index slot_of_prompt[p] // 2. `prompt_of`: of the 8 completions on one group index, at most 2 have prompts cached on any one group index, and on every group index some group index caches the prompts of exactly 2 of them.
All inputs are finite; a program needn't handle non-finite values.
Results may differ from a plain program's by a relative error of at most 0.012.
Values may be sent and summed in bfloat16 or wider, within the bound.
A program may use at most 128 MiB of HBM per device.

v0:
```python
import functools
import math

import numpy as np

import jax
import jax.numpy as jnp
from jax import lax
from jax.experimental import pallas as pl
from jax.experimental.pallas import tpu as pltpu
from jax.sharding import PartitionSpec as P

HEAD = 128
CAPC = 2
ROTARY_BASE = 1000000.0
TILE = 16
UNIT = 8
BATCH = 4
LANES = 128
MESH = pl.DeviceIdType.MESH
PIECES = 3
LEVELS = (
    (0.65625, 0.4375, 0.6875, 0.5625, 0.4286, 0.4286),
    (0.65625, 0.5, 0.75, 0.59375, 0.4571, 0.4571),
    (0.65625, 0.5625, 0.75, 0.625, 0.4857, 0.4857),
    (0.75, 0.5, 0.8125, 0.625, 0.4857, 0.4857),
    (0.75, 0.5625, 0.875, 0.6875, 0.5143, 0.5143),
    (0.84375, 0.65625, 0.9375, 0.75, 0.5429, 0.5429),
    (1, 1, 1, 1, 1.0000, 1.0000),
)


def rotary_tables(first_position, rows):
    half = HEAD // 2
    frequencies = np.float32(ROTARY_BASE) ** (
        -(np.arange(half, dtype=np.float32) * np.float32(2.0) / np.float32(HEAD))
    )
    positions = (first_position + np.arange(rows)).astype(np.float32)
    angles = (positions[:, None] * frequencies.astype(np.float32)[None, :]).astype(np.float64)
    cos, sin = np.cos(angles), np.sin(angles)
    return (
        np.concatenate([cos, cos], axis=1).astype(np.float32),
        np.concatenate([-sin, sin], axis=1).astype(np.float32),
    )


def padded_kernel(
    groups, lanes, moved,
    source_ref, tag_ref, dest_ref, length_ref,
    q_ref, k_ref, v_ref, cos_ref, sin_ref,
    out_ref,
    q_out, q_in, sel_out, sel_in, res, stage,
    q_send, q_recv, s_send, s_recv, r_send, r_recv,
    *near,
):
    me, lane = lax.axis_index("group"), lax.axis_index("tensor")
    held, rows, width = q_ref.shape
    cached, prefix, kv_width = k_ref.shape
    share = rows // lanes
    kv_local = kv_width // HEAD
    per_kv = width // HEAD // kv_local
    half = groups // 2
    factor = math.log2(math.e) / math.sqrt(HEAD)
    wide_near = moved * per_kv * HEAD
    if moved:
        (n_out, n_in, ns_out, ns_in, n_res, k_far, v_far,
         n_send, n_recv, ns_send, ns_recv, nr_send, nr_recv, kv_send, kv_recv) = near
    spot = lax.rem(me, half)
    base = me - spot
    mirror = lax.rem(me + half, groups)

    barrier = pltpu.get_barrier_semaphore()

    def greet(step, carry):
        for turn in range(lanes):
            def send():
                pl.semaphore_signal(
                    barrier, inc=1,
                    device_id=(lax.rem(me + step, groups), lax.rem(lane + turn, lanes)),
                    device_id_type=MESH,
                )
            if turn:
                send()
            else:
                pl.when(step > 0)(send)
        return carry

    lax.fori_loop(0, groups, greet, 0)

    def offset_of(step):
        swing = (step + 1) // 2
        return lax.rem(half + (1 - 2 * lax.rem(step, 2)) * swing + groups, groups)

    def route(owner):
        places = [owner * CAPC + slot for slot in range(CAPC)]
        return [(source_ref[place], tag_ref[place]) for place in places]

    def fill(items, q_to, sel_to, block, first, last):
        for slot, (item, tag) in enumerate(items):
            for j in range(cached):
                weight = jnp.where(tag == j, 1.0, 0.0)
                sel_to[block, slot * cached + j] = jnp.full(
                    (TILE, HEAD), weight, jnp.float32
                ).astype(jnp.bfloat16)
            for head in range(first, last):
                x = q_ref[item, :, head * HEAD:(head + 1) * HEAD].astype(jnp.float32)
                turned = x * cos_ref[...] + pltpu.roll(x, HEAD // 2, 1) * sin_ref[...]
                span = slice((head - first) * HEAD, (head - first + 1) * HEAD)
                q_to[block, slot, :, span] = turned.astype(jnp.bfloat16)

    near_heads, all_heads = moved * per_kv, width // HEAD

    def pair(src, dst, send_sem, recv_sem, device):
        return pltpu.make_async_remote_copy(
            src_ref=src, dst_ref=dst, send_sem=send_sem, recv_sem=recv_sem,
            device_id=device, device_id_type=MESH,
        )

    def q_copies(here, there, device):
        return (
            pair(sel_out.at[here], sel_in.at[there], s_send.at[here], s_recv.at[there],
                 (device, lane)),
            pair(q_out.at[here], q_in.at[there], q_send.at[here], q_recv.at[there],
                 (device, lane)),
        )

    def n_copies(here, there, device):
        return (
            pair(ns_out.at[here], ns_in.at[there], ns_send.at[here], ns_recv.at[there],
                 (device, lane)),
            pair(n_out.at[here], n_in.at[there], n_send.at[here], n_recv.at[there],
                 (device, lane)),
        )

    def place(owner, from_lane, skip, wide):
        start = pl.multiple_of(from_lane * width + skip, HEAD)
        return stage.at[pl.ds(owner * CAPC, CAPC), :, pl.ds(start, wide)]

    def r_copy(block, piece, owner, from_lane, device):
        return pair(
            res.at[block, :, piece], place(owner, from_lane, wide_near, width - wide_near),
            r_send.at[block, piece], r_recv.at[owner, from_lane], (device, piece),
        )

    def nr_copy(block, piece, owner, from_lane, device):
        return pair(
            n_res.at[block, :, piece], place(owner, from_lane, 0, wide_near),
            nr_send.at[block, piece], nr_recv.at[owner, from_lane], (device, piece),
        )

    def kv_copies():
        span = pl.ds(0, moved * HEAD)
        return (
            pair(k_ref.at[:, :, span], k_far, kv_send.at[0], kv_recv.at[0], (mirror, lane)),
            pair(v_ref.at[:, :, span], v_far, kv_send.at[1], kv_recv.at[1], (mirror, lane)),
        )

    items = route(mirror)
    fill(items, q_out, sel_out, mirror, near_heads, all_heads)
    pl.semaphore_wait(barrier, groups * lanes - 1)
    for copy in q_copies(mirror, me, mirror):
        copy.start()
    if moved:
        fill(items, n_in, ns_in, spot + half, 0, near_heads)

    def dispatch(step, carry):
        owner = lax.rem(me + offset_of(step), groups)
        items = route(owner)
        fill(items, q_out, sel_out, owner, near_heads, all_heads)
        for copy in q_copies(owner, me, owner):
            copy.start()
        if moved:
            fill(items, n_out, ns_out, owner, 0, near_heads)
            seat = lax.rem(owner, half)
            kind = lax.rem(lax.div(owner, half) + lax.div(me, half), 2)
            for copy in n_copies(owner, spot + half * kind, base + seat):
                copy.start()
        return carry

    lax.fori_loop(1, groups - 1, dispatch, 0)
    if moved:
        for copy in kv_copies():
            copy.start()
    items = route(me)
    fill(items, q_in, sel_in, me, near_heads, all_heads)
    if moved:
        fill(items, n_in, ns_in, spot, 0, near_heads)

    def attend(q_from, sel_from, to, block, keys, values, first, count):
        for slot in range(CAPC):
            weights = [sel_from[block, slot * cached + j][None] for j in range(cached)]

            def chosen(ref, span):
                total = None
                for j in range(cached):
                    part = ref[j, :, span].reshape(prefix // TILE, TILE, HEAD) * weights[j]
                    total = part if total is None else total + part
                return total.reshape(prefix, HEAD)

            for kv in range(count):
                span = slice((first + kv) * HEAD, (first + kv + 1) * HEAD)
                spans = [
                    slice((kv * per_kv + g) * HEAD, (kv * per_kv + g + 1) * HEAD)
                    for g in range(per_kv)
                ]
                query = jnp.concatenate([q_from[block, slot, :, s] for s in spans], axis=0)
                scores = lax.dot_general(
                    query, chosen(keys, span), (((1,), (1,)), ((), ())),
                    preferred_element_type=jnp.float32,
                )
                peak = jnp.max(scores, axis=-1, keepdims=True)
                weight = jnp.exp2((scores - peak) * factor)
                total = jnp.sum(weight, axis=-1, keepdims=True)
                mixed = jnp.dot(
                    weight.astype(jnp.bfloat16), chosen(values, span),
                    preferred_element_type=jnp.float32,
                )
                mixed = (mixed / total).astype(jnp.bfloat16)
                for g in range(per_kv):
                    to[block, slot, :, :, spans[g]] = mixed[g * rows:(g + 1) * rows].reshape(
                        lanes, share, HEAD
                    )

    def give_back(step, copy, source, block, owner, done, skip, wide):
        for turn in range(1, lanes):
            copy(block, lax.rem(lane + turn, lanes), owner, lane, source).start()

        @pl.when(step > 0)
        def _():
            copy(block, lane, owner, lane, source).start()

        @pl.when(step == 0)
        def _():
            start = pl.multiple_of(lane * width + skip, HEAD)
            stage[pl.ds(owner * CAPC, CAPC), :, pl.ds(start, wide)] = done[block, :, lane]

    def far_work(step, carry):
        source = lax.rem(me + groups - offset_of(lax.rem(step + groups - 1, groups)), groups)

        @pl.when(step > 0)
        def _():
            for copy in q_copies(source, source, source):
                copy.wait_recv()

        attend(q_in, sel_in, res, source, k_ref, v_ref, moved, kv_local - moved)
        give_back(step, r_copy, source, source, me, res, wide_near, width - wide_near)
        return carry

    def near_work(kind, keys, values, owner):
        def body(step, carry):
            seat = lax.rem(spot + step, half)
            block = seat + half * kind

            @pl.when(step > 0)
            def _():
                for copy in n_copies(block, block, base + seat):
                    copy.wait_recv()

            attend(n_in, ns_in, n_res, block, keys, values, 0, moved)
            give_back(step, nr_copy, base + seat, block, owner, n_res, 0, wide_near)
            return carry

        lax.fori_loop(0, half, body, 0)

    if moved:
        near_work(0, k_ref, v_ref, me)
    lax.fori_loop(0, groups, far_work, 0)
    if moved:
        for copy in kv_copies():
            copy.wait_recv()
        near_work(1, k_far, v_far, mirror)

    def returned(step, copy, block, owner, device):
        @pl.when(step > 0)
        def _():
            copy(block, lane, owner, lane, device).wait_send()
            copy(block, lane, owner, lane, device).wait_recv()

        for turn in range(1, lanes):
            piece = lax.rem(lane + turn, lanes)
            copy(block, piece, owner, piece, device).wait_send()
            copy(block, piece, owner, piece, device).wait_recv()

    def far_settle(step, carry):
        other = lax.rem(me + step, groups)

        @pl.when(step > 0)
        def _():
            for copy in q_copies(other, me, other):
                copy.wait_send()

        returned(step, r_copy, other, other, other)
        return carry

    lax.fori_loop(0, groups, far_settle, 0)
    if moved:
        for copy in kv_copies():
            copy.wait_send()

        def near_settle(step, carry):
            seat = lax.rem(spot + step, half)
            for kind in range(2):
                owner = lax.rem(base + half * kind, groups) + seat

                @pl.when(step > 0)
                def _():
                    for copy in n_copies(owner, owner, base + seat):
                        copy.wait_send()

                returned(step, nr_copy, seat + half * kind, owner, base + seat)
            return carry

        lax.fori_loop(0, half, near_settle, 0)

    def deliver(item, carry):
        found = stage[dest_ref[item]].astype(jnp.float32)
        position = lane * share + lax.broadcasted_iota(jnp.int32, found.shape, 0)
        out_ref[item] = jnp.where(position < length_ref[item], found, 0.0).astype(jnp.bfloat16)
        return carry

    lax.fori_loop(0, held, deliver, 0)


def padded(groups, lanes, queries, prefix_keys, prefix_values, slot_of_prompt, prompt_of, lengths):
    held, rows, width = queries.shape
    cached, prefix, kv_width = prefix_keys.shape
    share = rows // lanes
    kv_local = kv_width // HEAD
    moved = kv_local // 2 if groups % 2 == 0 and groups >= 4 else 0
    wide_near = moved * (width // kv_local)
    wide = width - wide_near
    cos, sin = rotary_tables(prefix, rows)
    cache_rows = slot_of_prompt[prompt_of]
    owner = cache_rows // cached
    serial = jnp.arange(held)
    earlier = (owner[None, :] == owner[:, None]) & (serial[None, :] < serial[:, None])
    destination = owner * CAPC + jnp.sum(earlier.astype(jnp.int32), axis=1)
    matches = destination[None, :] == jnp.arange(groups * CAPC)[:, None]
    source = jnp.sum(jnp.where(matches, serial[None, :], 0), axis=1)
    tags = jnp.sum(jnp.where(matches, (cache_rows % cached)[None, :], 0), axis=1)
    smem = pl.BlockSpec(memory_space=pltpu.SMEM)
    vmem = pl.BlockSpec(memory_space=pltpu.VMEM)
    dma = pltpu.SemaphoreType.DMA
    bf16 = jnp.bfloat16

    def exchange(features):
        return [
            pltpu.VMEM((groups, CAPC, rows, features), bf16),
            pltpu.VMEM((groups, CAPC, rows, features), bf16),
            pltpu.VMEM((groups, CAPC * cached, TILE, HEAD), bf16),
            pltpu.VMEM((groups, CAPC * cached, TILE, HEAD), bf16),
            pltpu.VMEM((groups, CAPC, lanes, share, features), bf16),
        ]

    semaphores = [
        dma((groups,)), dma((groups,)),
        dma((groups,)), dma((groups,)),
        dma((groups, lanes)), dma((groups, lanes)),
    ]
    scratch = [
        *exchange(wide),
        pltpu.VMEM((groups * CAPC, share, width * lanes), bf16),
        *semaphores,
    ]
    if moved:
        scratch += [
            *exchange(wide_near),
            pltpu.VMEM((cached, prefix, moved * HEAD), bf16),
            pltpu.VMEM((cached, prefix, moved * HEAD), bf16),
            *semaphores,
            dma((2,)), dma((2,)),
        ]
    return pl.pallas_call(
        functools.partial(padded_kernel, groups, lanes, moved),
        out_shape=jax.ShapeDtypeStruct((held, share, width * lanes), bf16),
        in_specs=[smem] * 4 + [vmem] * 5,
        out_specs=vmem,
        scratch_shapes=scratch,
        compiler_params=pltpu.CompilerParams(collective_id=0, has_side_effects=True),
        name="routed_prefix_attention",
    )(
        source.astype(jnp.int32), tags.astype(jnp.int32), destination.astype(jnp.int32), lengths,
        queries, prefix_keys, prefix_values, jnp.asarray(cos), jnp.asarray(sin),
    )


def xor_order(step, plane, planes):
    half = planes // 2
    near = lax.div(step, half)
    side = lax.rem(lax.div(plane, half) + 1 - near, 2)
    return side * half + lax.rem(lax.rem(plane, half) + step + near, half)


def step_of(plane, z, planes):
    half = planes // 2
    shift = lax.rem(plane + planes - z, half)
    far = shift
    near = half + lax.rem(shift + half - 1, half)
    return jnp.where(plane // half != z // half, far, near)


def plan_kernel(
    groups, pair, levels, full, base,
    slot_ref, prompt_ref, length_ref, q_ref, k_ref, v_ref, cos_ref, sin_ref,
    tables_ref, level_ref, k_far, v_far, q_base,
    mine, gathered, q_out, send, recv, q_send, q_recv, kv_send, kv_recv,
):
    shared = len(base)
    me, lane = lax.axis_index("group"), lax.axis_index("tensor")
    held = prompt_ref.shape[0]
    slots = slot_ref.shape[0]
    planes = groups // pair
    per_plane = slots // planes
    total = groups * held
    full_pair, full_plane = full
    turns = full_pair // (CAPC * pair)
    half = planes // 2
    z, x = lax.div(me, pair), lax.rem(me, pair)
    partner = z * pair + 1 - x
    there = [xor_order(step, z, planes) for step in range(shared)]
    barrier = pltpu.get_barrier_semaphore()

    def greet(step, carry):
        pl.semaphore_signal(
            barrier, inc=1, device_id=(lax.rem(me + step, groups), lane), device_id_type=MESH
        )
        return carry

    lax.fori_loop(1, groups, greet, 0)

    def remote(src, dst, send_sem, recv_sem, group):
        return pltpu.make_async_remote_copy(
            src_ref=src, dst_ref=dst, send_sem=send_sem, recv_sem=recv_sem,
            device_id=(group, lane), device_id_type=MESH,
        )

    span = pl.ds(pl.multiple_of((1 - x) * HEAD, HEAD), HEAD)
    kv_copies = [
        remote(ref.at[:, :, span], far_ref, kv_send.at[i], kv_recv.at[i], partner)
        for i, (ref, far_ref) in enumerate(((k_ref, k_far), (v_ref, v_far)))
    ]

    def q_copy(step, j, source, device):
        return remote(
            q_out.at[step, j, pl.ds(0, base[step])], q_base.at[step, source, pl.ds(0, base[step])],
            q_send.at[step, j], q_recv.at[step, source], device,
        )

    own_slots = [slot_ref[prompt_ref[i]] for i in range(held)]
    own_planes = [lax.div(slot, per_plane) for slot in own_slots]
    own_counts = [lax.div(length_ref[i] + UNIT - 1, UNIT) for i in range(held)]
    own_starts = []
    for i in range(held):
        start = jnp.int32(0)
        for other in range(i):
            start = start + jnp.where(own_planes[other] == own_planes[i], own_counts[other], 0)
        own_starts.append(start)

    def fill(step):
        starts = [
            jnp.where(own_planes[i] == there[step], own_starts[i], LANES) for i in range(held)
        ]

        def one(k, carry):
            index = jnp.int32(0)
            for i in range(held):
                offset = k - starts[i]
                hit = (offset >= 0) & (offset < own_counts[i])
                index = index + jnp.where(hit, i * turns + offset, 0)
            rope(index, q_ref, cos_ref, sin_ref, q_out.at[step], k, pair)
            return carry

        lax.fori_loop(0, base[step], one, 0)

    lanes1 = lax.broadcasted_iota(jnp.int32, (1, LANES), 1)
    row = jnp.zeros((1, LANES), jnp.int32)
    for i in range(held):
        value = own_slots[i] * LANES + length_ref[i]
        row = jnp.where(lanes1 == me * held + i, value, row)
    mine[...] = row
    gathered[me] = row
    for step in range(half):
        fill(step)
    pl.semaphore_wait(barrier, groups - 1)

    def copy(there, device):
        return pltpu.make_async_remote_copy(
            src_ref=mine, dst_ref=gathered.at[there], send_sem=send.at[device],
            recv_sem=recv.at[there], device_id=(device, lane), device_id_type=MESH,
        )

    def push(step, carry):
        copy(me, lax.rem(me + step, groups)).start()
        return carry

    lax.fori_loop(1, groups, push, 0)

    def dispatch(step):
        for j in range(pair):
            q_copy(step, j, x, there[step] * pair + j).start()

    for step in range(half):
        dispatch(step)
    for kv_copy in kv_copies:
        kv_copy.start()
    for step in range(half, shared):
        fill(step)
        dispatch(step)

    def settle(step, carry):
        other = lax.rem(me + step, groups)
        copy(other, other).wait_recv()
        copy(me, other).wait_send()
        return carry

    lax.fori_loop(1, groups, settle, 0)
    code = gathered[0]
    for g in range(1, groups):
        code = code + gathered[g]

    square = (LANES, LANES)
    down = lax.broadcasted_iota(jnp.int32, square, 0)
    across = lax.broadcasted_iota(jnp.int32, square, 1)
    eye = down == across

    def to_column(values):
        return jnp.sum(jnp.where(eye, jnp.broadcast_to(values, square), 0), axis=1, keepdims=True)

    def to_row(values):
        return jnp.sum(jnp.where(eye, jnp.broadcast_to(values, square), 0), axis=0, keepdims=True)

    def facts(values, index):
        live = index < total
        length = values % LANES
        slot = values // LANES
        count = jnp.where(live, (length + UNIT - 1) // UNIT, 0)
        return count, slot, slot // per_plane, index // held, index // (held * pair)

    col = to_column(code)
    down1 = lax.broadcasted_iota(jnp.int32, (LANES, 1), 0)
    count_r, slot_r, to_r, from_r, plane_r = facts(code, lanes1)
    count_c, slot_c, to_c, from_c, plane_c = facts(col, down1)
    weight = jnp.broadcast_to(count_c, square)
    earlier = (down < across) & (to_c == to_r)

    def rank(mask):
        return jnp.sum(jnp.where(mask, weight, 0), axis=0, keepdims=True)

    base1 = rank(earlier & (from_c == from_r))
    base2 = rank(earlier & (plane_c == plane_r))
    side_r = jnp.where(plane_r // half == to_r // half, 1, 0)
    side_c = jnp.where(plane_c // half == to_c // half, 1, 0)
    within = rank(earlier & (side_c == side_r) & (slot_c == slot_r))
    key_r = side_r * slots + slot_r
    number = jnp.sum(
        jnp.where(down1 == key_r, jnp.broadcast_to(count_r, square), 0), axis=1, keepdims=True
    )
    need = (number + BATCH - 1) // BATCH
    need_r = to_row(need)
    first = jnp.sum(
        jnp.where(
            (down // per_plane == across // per_plane) & (across < down),
            jnp.broadcast_to(need_r, square), 0,
        ),
        axis=1, keepdims=True,
    )
    first_of = jnp.sum(
        jnp.where(down1 == key_r, jnp.broadcast_to(first, square), 0), axis=0, keepdims=True
    )
    place = first_of * BATCH + within
    base1_c, base2_c, place_c = to_column(base1), to_column(base2), to_column(place)

    alive = lanes1 < total
    far = alive & (to_r // half != plane_r // half)
    near = alive & (to_r // half == plane_r // half)
    needs = [
        jnp.max(jnp.where(mask, begin + count_r, 0))
        for mask in (far, near) for begin in (base1, base2)
    ] + [jnp.max(jnp.where(down1 // slots == side, first + need, 0)) for side in range(2)]
    level = jnp.int32(len(levels) - 1)
    for index, caps in reversed(list(enumerate(levels[:-1]))):
        over = needs[0] > caps[0]
        for value, cap in zip(needs[1:], caps[1:]):
            over = over | (value > cap)
        level = jnp.where(over, level, index)
    level_ref[0] = level
    tables_ref[pl.ds(1, 1), :] = code
    tables_ref[pl.ds(2, 1), :] = step_of(to_r, z, planes) * full_plane + base2

    def pick(mask, start_c, value_c, index):
        hit = mask & (index >= start_c) & (index < start_c + count_c)
        return jnp.sum(jnp.where(hit, value_c + index, 0), axis=0, keepdims=True)

    for plane in range(planes):
        tables_ref[pl.ds(3 + plane, 1), :] = pick(
            (from_c == me) & (to_c == plane), base1_c,
            lax.rem(down1, held) * turns - base1_c, lanes1,
        )
        tables_ref[pl.ds(3 + planes + plane, 1), :] = pick(
            (plane_c == plane) & (to_c == z), base2_c, place_c - base2_c, lanes1
        )
    seat_c = lax.rem(step_of(plane_c, z, planes), half) * pair + lax.rem(from_c, pair)
    for side in range(2):
        for page in range(2):
            tables_ref[pl.ds(3 + 2 * planes + 2 * side + page, 1), :] = pick(
                (side_c == side) & (to_c == z), place_c,
                seat_c * full_pair + base1_c - place_c, lanes1 + page * LANES,
            )
        starts = (
            (down1 // slots == side) & (lax.rem(down1, slots) // per_plane == z)
            & (lanes1 >= first) & (lanes1 < first + need)
        )
        tables_ref[pl.ds(7 + 2 * planes + side, 1), :] = jnp.sum(
            jnp.where(starts, lax.rem(down1, per_plane), 0), axis=0, keepdims=True
        )
    for step in range(shared):
        for j in range(pair):
            q_copy(step, j, j, me).wait_recv()
            q_copy(step, j, x, there[step] * pair + j).wait_send()
    for kv_copy in kv_copies:
        kv_copy.wait_recv()
        kv_copy.wait_send()


def rope(index, q_ref, cos_ref, sin_ref, to, k, pair):
    turn = lax.rem(index, cos_ref.shape[0])
    cos, sin = cos_ref[turn], sin_ref[turn]
    block = q_ref[index].astype(jnp.float32)
    per_kv = block.shape[-1] // HEAD // pair
    for j in range(pair):
        parts = []
        for g in range(per_kv):
            head = j * per_kv + g
            part = block[:, head * HEAD:(head + 1) * HEAD]
            turned = part * cos + pltpu.roll(part, HEAD // 2, 1) * sin
            parts.append(turned.astype(jnp.bfloat16))
        to[j, k] = jnp.concatenate(parts, axis=1)


def packed_kernel(
    groups, lanes, pair, full, caps, cuts, base,
    tables,
    q_ref, k_ref, v_ref, k_far, v_far, q_base, cos_ref, sin_ref,
    out_ref,
    *scratch,
):
    me, lane = lax.axis_index("group"), lax.axis_index("tensor")
    planes = groups // pair
    half = planes // 2
    pieces = len(cuts)
    scratch = list(scratch)

    def take(count):
        taken = scratch[:count]
        del scratch[:count]
        return taken

    q_out, q_sides, results = take(planes), take(2), take(2)
    q_in = [q_sides[step // half].at[step % half] for step in range(planes)]
    r_out, r_in, stage = take(pieces), take(pieces), take(pieces)
    k_all, v_all = take(2)
    q_send, q_recv, kv_here, q_here, r_send, r_recv, f_send, f_recv = scratch

    z, x = lax.div(me, pair), lax.rem(me, pair)
    cached, prefix, _ = k_ref.shape
    units, _, width = q_ref.shape
    wide = width // pair
    per_kv = wide // HEAD
    turns = cos_ref.shape[0]
    held = units // turns
    share = turns // lanes
    full_pair, full_plane = full
    cap1, cap2, near1, near2 = caps[:4]
    factor = math.log2(math.e) / math.sqrt(HEAD)
    send_row, ret_row, comp_row, slot_row = 3, 3 + planes, 3 + 2 * planes, 7 + 2 * planes
    counts1 = [cap1 if step < half else near1 for step in range(planes)]
    counts2 = [cap2 if step < half else near2 for step in range(planes)]
    offsets = [sum(counts2[:step]) for step in range(planes)]
    last = planes - 1
    there = [xor_order(step, z, planes) for step in range(planes)]

    barrier = pltpu.get_barrier_semaphore()

    def greet(step, carry):
        pl.semaphore_signal(
            barrier, inc=1, device_id=(lax.rem(me + step, groups), lane), device_id_type=MESH
        )
        return carry

    lax.fori_loop(1, groups, greet, 0)
    for turn in range(1, lanes):
        for j in range(pair):
            pl.semaphore_signal(
                barrier, inc=1,
                device_id=(z * pair + j, lax.rem(lane + turn, lanes)), device_id_type=MESH,
            )

    def span_of(j):
        return pl.ds(pl.multiple_of(j * HEAD, HEAD), HEAD)

    here = [
        pltpu.make_async_copy(
            ref.at[:, :, span_of(x)], full_ref.at[pl.ds(x * cached, cached)], kv_here.at[i]
        )
        for i, (ref, full_ref) in enumerate(((k_ref, k_all), (v_ref, v_all)))
    ] + [
        pltpu.make_async_copy(
            far_ref, full_ref.at[pl.ds((1 - x) * cached, cached)], kv_here.at[2 + i]
        )
        for i, (far_ref, full_ref) in enumerate(((k_far, k_all), (v_far, v_all)))
    ] + [
        pltpu.make_async_copy(
            q_base.at[step, :, pl.ds(0, base[step])], q_in[step].at[:, pl.ds(0, base[step])],
            q_here.at[step],
        )
        for step in range(len(base))
    ]
    for copy in here:
        copy.start()

    def remote(src, dst, send_sem, recv_sem, group, to_lane):
        return pltpu.make_async_remote_copy(
            src_ref=src, dst_ref=dst, send_sem=send_sem, recv_sem=recv_sem,
            device_id=(group, to_lane), device_id_type=MESH,
        )

    rest = [
        slice(base[step] if step < len(base) else 0, counts1[step]) for step in range(planes)
    ]

    def q_copy(step, j, source, device):
        span = pl.ds(rest[step].start, rest[step].stop - rest[step].start)
        return remote(
            q_out[step].at[j, span], q_in[step].at[source, span], q_send.at[step, j],
            q_recv.at[step, source], device, lane,
        )

    def fill(step):
        def one(k, carry):
            index = tables[send_row + there[step], k]
            rope(index, q_ref, cos_ref, sin_ref, q_out[step], k, pair)
            return carry

        lax.fori_loop(rest[step].start, rest[step].stop, one, 0)

    moving = [step for step in range(planes) if rest[step].stop > rest[step].start]

    def dispatch(step):
        if step not in moving:
            return
        for j in range(pair):
            if step < last:
                q_copy(step, j, x, there[step] * pair + j).start()
            else:
                @pl.when(j != x)
                def _():
                    q_copy(step, j, x, there[step] * pair + j).start()

    for step in moving:
        fill(step)
    q_in[last][x] = q_out[last][x]

    def greeted():
        pl.semaphore_wait(barrier, groups - 1 + pair * (lanes - 1))
        for step in moving:
            dispatch(step)

    if 0 in moving:
        greeted()
    for copy in here:
        copy.wait()

    def r_copy(piece, step):
        region = pl.ds(offsets[step], counts2[step])
        return remote(
            r_out[piece].at[region], r_in[piece].at[region],
            r_send.at[piece, step], r_recv.at[piece, step], there[step] * pair + x, lane,
        )

    for side in range(2):
        steps = range(side * half, side * half + half)
        for step in steps:
            for j in range(pair) if step in moving else []:
                if step < last:
                    q_copy(step, j, j, me).wait_recv()
                else:
                    @pl.when(j != x)
                    def _():
                        q_copy(step, j, j, me).wait_recv()

        def batch(b, carry):
            slot = tables[slot_row + side, b]
            blocks = []
            for i in range(BATCH):
                entry = b * BATCH + i
                index = tables[
                    comp_row + 2 * side + lax.div(entry, LANES), lax.rem(entry, LANES)
                ]
                seat = lax.div(index, full_pair)
                blocks.append(
                    q_sides[side][
                        lax.div(seat, pair), lax.rem(seat, pair), lax.rem(index, full_pair)
                    ].astype(jnp.float32)
                )
            query = jnp.concatenate(
                [block[:, g * HEAD:(g + 1) * HEAD] for g in range(per_kv) for block in blocks],
                axis=0,
            ).astype(jnp.bfloat16)
            scores = lax.dot_general(
                query, k_all[slot], (((1,), (1,)), ((), ())), preferred_element_type=jnp.float32
            )
            peak = jnp.max(scores, axis=-1, keepdims=True)
            weight = jnp.exp2((scores - peak) * factor)
            total = jnp.sum(weight, axis=-1, keepdims=True)
            mixed = jnp.dot(
                weight.astype(jnp.bfloat16), v_all[slot], preferred_element_type=jnp.float32
            ) / total
            for i in range(BATCH):
                results[side][b * BATCH + i] = jnp.concatenate(
                    [
                        mixed[(g * BATCH + i) * UNIT:(g * BATCH + i + 1) * UNIT]
                        for g in range(per_kv)
                    ],
                    axis=1,
                ).astype(jnp.bfloat16)
            return carry

        lax.fori_loop(0, results[side].shape[0] // BATCH, batch, 0, unroll=2)
        if side == 0 and 0 not in moving:
            greeted()
        for step in steps:
            target = r_out if step < last else r_in

            def pack(k, carry):
                found = results[side][tables[ret_row + there[step], k]]
                start = 0
                for piece in range(pieces):
                    target[piece][offsets[step] + k] = found[:, start:start + cuts[piece]]
                    start += cuts[piece]
                return carry

            lax.fori_loop(0, counts2[step], pack, 0, unroll=2)
            if step < last:
                r_copy(0, step).start()
            if step == half - 1:
                for piece in range(1, pieces):
                    for ready in range(half):
                        r_copy(piece, ready).start()
            if step == last - 1:
                for piece in range(1, pieces):
                    for ready in range(half, last):
                        r_copy(piece, ready).start()

    def lineup(step):
        return lax.rem(x + step + 1, pair), lax.rem(lane + lax.div(step + 1, pair), lanes)

    def final(piece, at_x, at_lane, from_x, from_lane, to_x, to_lane):
        skip = sum(cuts[:piece])
        start = pl.multiple_of((from_lane * pair + from_x) * wide + skip, HEAD)
        return remote(
            stage[piece].at[at_x, at_lane], out_ref.at[:, :, pl.ds(start, cuts[piece])],
            f_send.at[piece, at_x, at_lane], f_recv.at[piece, from_x, from_lane],
            z * pair + to_x, to_lane,
        )

    for piece in range(pieces):
        for step in range(last):
            r_copy(piece, step).wait_recv()

        def spread(step, carry):
            to_x, to_lane = lineup(step)

            def one(i, inner):
                item = (z * pair + to_x) * held + i
                entry = tables[2, item]
                length = lax.rem(tables[1, item], LANES)
                source, rank = lax.div(entry, full_plane), lax.rem(entry, full_plane)
                cap = jnp.where(source < half, cap2, near2)
                offset = jnp.where(
                    source < half, source * cap2, half * cap2 + (source - half) * near2
                )
                for s in range(share):
                    unit = to_lane * share + s
                    found = r_in[piece][offset + jnp.minimum(rank + unit, cap - 1)].astype(
                        jnp.float32
                    )
                    row = unit * UNIT + lax.broadcasted_iota(jnp.int32, found.shape, 0)
                    stage[piece][to_x, to_lane, i * share + s] = jnp.where(
                        row < length, found, 0.0
                    ).astype(jnp.bfloat16)
                return inner

            lax.fori_loop(0, held, one, 0, unroll=2)

            @pl.when(step < pair * lanes - 1)
            def _():
                final(piece, to_x, to_lane, x, lane, to_x, to_lane).start()
            return carry

        lax.fori_loop(0, pair * lanes, spread, 0)
        start = pl.multiple_of((lane * pair + x) * wide + sum(cuts[:piece]), HEAD)
        out_ref[:, :, pl.ds(start, cuts[piece])] = stage[piece][x, lane]

    def drain(step, carry):
        to_x, to_lane = lineup(step)
        for piece in range(pieces):
            final(piece, to_x, to_lane, to_x, to_lane, to_x, to_lane).wait_recv()
            final(piece, to_x, to_lane, x, lane, to_x, to_lane).wait_send()
        return carry

    lax.fori_loop(0, pair * lanes - 1, drain, 0)
    for step in range(planes):
        for j in range(pair) if step in moving else []:
            if step < last:
                q_copy(step, j, x, there[step] * pair + j).wait_send()
            else:
                @pl.when(j != x)
                def _():
                    q_copy(step, j, x, there[step] * pair + j).wait_send()
        if step < last:
            for piece in range(pieces):
                r_copy(piece, step).wait_send()


def packed(groups, lanes, queries, prefix_keys, prefix_values, slot_of_prompt, prompt_of, lengths):
    held, rows, width = queries.shape
    cached, prefix, kv_width = prefix_keys.shape
    pair = kv_width // HEAD
    planes = groups // pair
    half = planes // 2
    turns = rows // UNIT
    full_pair = CAPC * pair * turns
    full_plane = full_pair * pair
    slots = cached * pair
    full_side = (full_plane * half + slots * (BATCH - 1)) // BATCH
    share = turns // lanes
    wide = width // pair
    per_kv = wide // HEAD
    cuts = [HEAD * (per_kv // PIECES + (i < per_kv % PIECES)) for i in range(PIECES)]
    levels = [
        tuple(
            round(whole * part)
            for whole, part in zip((full_pair, full_plane) * 2 + (full_side, full_side), level)
        )
        for level in LEVELS
    ]
    smem = pl.BlockSpec(memory_space=pltpu.SMEM)
    vmem = pl.BlockSpec(memory_space=pltpu.VMEM)
    anywhere = pl.BlockSpec(memory_space=pl.ANY)
    dma = pltpu.SemaphoreType.DMA
    bf16 = jnp.bfloat16
    table_rows = -(-(9 + 2 * planes) // 8) * 8
    full = (full_pair, full_plane)
    cos, sin = (jnp.asarray(table.reshape(turns, UNIT, HEAD)) for table in rotary_tables(prefix, rows))
    units = queries.reshape(held * turns, UNIT, width)
    base = [min(level[0] for level in levels)] * half
    base += [min(level[2] for level in levels)] * (planes - half - 1)
    base_shape = (len(base), pair, max(base), UNIT, wide)
    far_shape = jax.ShapeDtypeStruct((cached, prefix, HEAD), bf16)
    tables, chosen, k_far, v_far, q_base = pl.pallas_call(
        functools.partial(plan_kernel, groups, pair, levels, full, base),
        out_shape=[
            jax.ShapeDtypeStruct((table_rows, LANES), jnp.int32),
            jax.ShapeDtypeStruct((1,), jnp.int32),
            far_shape, far_shape,
            jax.ShapeDtypeStruct(base_shape, bf16),
        ],
        in_specs=[smem] * 3 + [vmem, anywhere, anywhere, vmem, vmem],
        out_specs=[vmem, smem] + [anywhere] * 3,
        scratch_shapes=[
            pltpu.VMEM((1, LANES), jnp.int32),
            pltpu.VMEM((groups, 1, LANES), jnp.int32),
            pltpu.VMEM(base_shape, bf16),
            dma((groups,)), dma((groups,)),
            dma((len(base), pair)), dma((len(base), pair)), dma((2,)), dma((2,)),
        ],
        compiler_params=pltpu.CompilerParams(collective_id=1, has_side_effects=True),
        name="plan_and_share",
    )(slot_of_prompt, prompt_of, lengths, units, prefix_keys, prefix_values, cos, sin)
    operands = (tables, units, prefix_keys, prefix_values, k_far, v_far, q_base, cos, sin)

    def branch(level):
        cap1, cap2, near1, near2, *batches = caps = levels[level]
        counts1 = [cap1] * half + [near1] * half
        counts2 = [cap2] * half + [near2] * half

        def run(*values):
            return pl.pallas_call(
                functools.partial(packed_kernel, groups, lanes, pair, full, caps, cuts, base),
                out_shape=jax.ShapeDtypeStruct((held * share, UNIT, width * lanes), bf16),
                in_specs=[smem, vmem] + [anywhere] * 5 + [vmem, vmem],
                out_specs=vmem,
                scratch_shapes=[
                    *(pltpu.VMEM((pair, count, UNIT, wide), bf16) for count in counts1),
                    *(pltpu.VMEM((half, pair, count, UNIT, wide), bf16) for count in (cap1, near1)),
                    *(pltpu.VMEM((count * BATCH, UNIT, wide), bf16) for count in batches),
                    *(pltpu.VMEM((sum(counts2), UNIT, cut), bf16) for cut in cuts),
                    *(pltpu.VMEM((sum(counts2), UNIT, cut), bf16) for cut in cuts),
                    *(pltpu.VMEM((pair, lanes, held * share, UNIT, cut), bf16) for cut in cuts),
                    pltpu.VMEM((slots, prefix, HEAD), bf16),
                    pltpu.VMEM((slots, prefix, HEAD), bf16),
                    dma((planes, pair)), dma((planes, pair)), dma((4,)), dma((len(base),)),
                    dma((PIECES, planes)), dma((PIECES, planes)),
                    dma((PIECES, pair, lanes)), dma((PIECES, pair, lanes)),
                ],
                compiler_params=pltpu.CompilerParams(
                    collective_id=2 + level, has_side_effects=True
                ),
                name=f"packed_prefix_attention_{level}",
            )(*values)

        return run

    out = lax.switch(
        chosen.reshape(()), [branch(level) for level in range(len(levels))], *operands
    )
    return out.reshape(held, share * UNIT, width * lanes)


def fits(groups, lanes, queries, prefix_keys):
    held, rows, width = queries.shape
    pair = prefix_keys.shape[2] // HEAD
    if pair != 2 or groups // pair not in (2, 4) or groups % (2 * pair):
        return False
    if rows % (UNIT * lanes) or rows >= LANES:
        return False
    slots = pair * prefix_keys.shape[0]
    spots = 2 * groups * prefix_keys.shape[0]
    full_plane = CAPC * pair * pair * rows // UNIT
    room = groups // pair // 2 * full_plane + slots * (BATCH - 1)
    return max(groups * held, spots, full_plane) <= LANES and room <= 2 * LANES


def local(groups, lanes, queries, prefix_keys, *rest):
    form = packed if fits(groups, lanes, queries, prefix_keys) else padded
    return form(groups, lanes, queries, prefix_keys, *rest)


def solution(mesh):
    placed = (
        P("group", None, "tensor"),
        P("group", None, "tensor"),
        P("group", None, "tensor"),
        P(),
        P("group"),
        P("group"),
    )
    return jax.shard_map(
        functools.partial(local, mesh.shape["group"], mesh.shape["tensor"]),
        mesh=mesh, in_specs=placed, out_specs=P("group", "tensor", None), check_vma=False,
    )
```

profile of v0, /device:TPU:0, one launch (start us, length us, event | category | flops | bytes accessed | tf_op | source)
XLA Modules:
  0.0 122.2 jit_solution(13798053809458091148)
XLA Ops:
  0.0 0.0 copy-start
  0.0 0.0 copy-start.1
  0.0 0.0 copy-start.2
  0.0 0.0 copy-start.3
  0.0 0.0 copy-start.4
  0.0 46.5 %plan_and_share.1 = (s32[24,128]{1,0:T(8,128)S(1)}, s32[1]{0:T(128)}, bf16[2,1024,128]{2,1,0:T(8,128)(2,1)}, bf16[2,1024,128]{2,1,0:T(8,128)(2,1)}, bf16[3,2,22,8,640]{4,3,2,1,0:T(8,128)(2,1)}) custom-call(s32[16]{0:T(128)} %slot_ref.1, s32[8]{0:T(128)} %prompt_ref.1, s32[8]{0:T(128)} %length_ref.1, bf16[64,8,1280]{2,1,0:T(8,128)(2,1)} %bitcast.9, ...), custom_call_target="tpu_custom_call" | custom-call | tf_op jit(solution)/shard_map/plan_and_share/pallas_call | solution.py:960
  47.2 0.0 copy-done
  47.2 0.0 copy-done.1
  47.2 0.0 copy-done.2
  47.2 0.0 copy-done.3
  47.2 0.0 copy-done.4
  47.3 72.5 %conditional.1 = (bf16[8,16,5120]{2,1,0:T(8,128)(2,1)}) conditional(s32[]{:T(128)} %bitcast.8, (s32[24,128]{1,0:T(8,128)S(1)}, bf16[64,8,1280]{2,1,0:T(8,128)(2,1)S(1)}, bf16[2,1024,256]{2,1,0:T(8,128)(2,1)S(1)}, bf16[2,1024,256]{2,1,0:T(8,128)(2,1)S(1)}, bf16[2,1024,128]{2,1,0:T(8,128)(2,1)}, ...), branch_computations={%region_0.0_spmd, %region_1.0_spmd, %region_2.0_spmd, %region_3.0_... | conditional | bytes 8 | solution.py:1014
  47.5 72.0 %packed_prefix_attention_5.1 = bf16[16,8,5120]{2,1,0:T(8,128)(2,1)} custom-call(s32[24,128]{1,0:T(8,128)S(1)} %get-tuple-element.185.tables, bf16[64,8,1280]{2,1,0:T(8,128)(2,1)S(1)} %get-tuple-element.186.q_ref, bf16[2,1024,256]{2,1,0:T(8,128)(2,1)S(1)} %get-tuple-element.187.k_ref, bf16[2,1024,256]{2,1,0:T(8,128)(2,1)S(1)} %get-tuple-element.188.v_ref, ...), custom_call_target="tpu_custom_call" | custom-call | tf_op jit(solution)/shard_map/cond/branch_5_fun/packed_prefix_attention_5/pallas_call | solution.py:988
  119.7 2.5 %copy.24 = bf16[8,16,5120]{2,1,0:T(8,128)(2,1)} copy(bf16[8,16,5120]{2,1,0:T(8,128)(2,1)} %get-tuple-element.213) | data formatting | bytes 2621440
Async XLA Ops:
  0.0 47.2 %copy-start = (bf16[8,64,1280]{2,1,0:T(8,128)(2,1)S(1)}, bf16[8,64,1280]{2,1,0:T(8,128)(2,1)}, u32[]{:S(2)}) copy-start(bf16[8,64,1280]{2,1,0:T(8,128)(2,1)} %param.15) | copy-start | bytes 3932164
  0.0 47.2 %copy-start.1 = (bf16[2,1024,256]{2,1,0:T(8,128)(2,1)S(1)}, bf16[2,1024,256]{2,1,0:T(8,128)(2,1)}, u32[]{:S(2)}) copy-start(bf16[2,1024,256]{2,1,0:T(8,128)(2,1)} %k_ref.1) | copy-start | bytes 3145732
  0.0 47.2 %copy-start.2 = (bf16[2,1024,256]{2,1,0:T(8,128)(2,1)S(1)}, bf16[2,1024,256]{2,1,0:T(8,128)(2,1)}, u32[]{:S(2)}) copy-start(bf16[2,1024,256]{2,1,0:T(8,128)(2,1)} %v_ref.1) | copy-start | bytes 3145732
  0.0 47.2 %copy-start.3 = (f32[8,8,128]{2,1,0:T(8,128)S(1)}, f32[8,8,128]{2,1,0:T(8,128)}, u32[]{:S(2)}) copy-start(f32[8,8,128]{2,1,0:T(8,128)} %constant.11.clone.sin_ref) | copy-start | bytes 98308
  0.0 47.2 %copy-start.4 = (f32[8,8,128]{2,1,0:T(8,128)S(1)}, f32[8,8,128]{2,1,0:T(8,128)}, u32[]{:S(2)}) copy-start(f32[8,8,128]{2,1,0:T(8,128)} %constant.10.clone.cos_ref) | copy-start | bytes 98308
where the time goes:
time: 122 us
  Pallas kernels  118 us (97%)
  local copies, waits for them, and re-layouts  2.48 us (2%)
    pallas_call x1, Pallas kernels, run(): pl.pallas_call(functools.partial(packed_kernel, groups, lanes, pair, full...  72 us
    pallas_call x1, Pallas kernels, packed(): pl.pallas_call(functools.partial(plan_kernel, groups, pair, levels, full,...  46.5 us
    unnamed x11, local copies, waits for them, and re-layouts  2.48 us

commit v1 on v0

--- a/solution.py
+++ b/solution.py
@@ -19,6 +19,7 @@
 LANES = 128
 MESH = pl.DeviceIdType.MESH
 PIECES = 3
+ROOM = 28 * 2**20
 LEVELS = (
     (0.65625, 0.4375, 0.6875, 0.5625, 0.4286, 0.4286),
     (0.65625, 0.5, 0.75, 0.59375, 0.4571, 0.4571),
@@ -974,7 +975,9 @@
             dma((groups,)), dma((groups,)),
             dma((len(base), pair)), dma((len(base), pair)), dma((2,)), dma((2,)),
         ],
-        compiler_params=pltpu.CompilerParams(collective_id=1, has_side_effects=True),
+        compiler_params=pltpu.CompilerParams(
+            collective_id=1, has_side_effects=True, vmem_limit_bytes=ROOM
+        ),
         name="plan_and_share",
     )(slot_of_prompt, prompt_of, lengths, units, prefix_keys, prefix_values, cos, sin)
     operands = (tables, units, prefix_keys, prefix_values, k_far, v_far, q_base, cos, sin)
@@ -1004,7 +1007,7 @@
                     dma((PIECES, pair, lanes)), dma((PIECES, pair, lanes)),
                 ],
                 compiler_params=pltpu.CompilerParams(
-                    collective_id=2 + level, has_side_effects=True
+                    collective_id=2 + level, has_side_effects=True, vmem_limit_bytes=ROOM
                 ),
                 name=f"packed_prefix_attention_{level}",
             )(*values)

time: 122 us -> 104 us (0.85)
  Pallas kernels: 118 us -> 99.5 us
    pallas_call x1, Pallas kernels: 72 us -> 53.1 us  [run(): pl.pallas_call(functools.partial(packed_kernel, groups, lanes, pair, full...]
    unnamed x11 -> x17, local copies, waits for them, and re-layouts: 2.48 us -> 3.04 us
where the time goes in v1:
time: 104 us
  Pallas kernels  99.5 us (96%)
  local copies, waits for them, and re-layouts  3.04 us (3%)
    pallas_call x1, Pallas kernels, run(): pl.pallas_call(functools.partial(packed_kernel, groups, lanes, pair, full...  53.1 us
    pallas_call x1, Pallas kernels, packed(): pl.pallas_call(functools.partial(plan_kernel, groups, pair, levels, full,...  46.4 us
    unnamed x17, local copies, waits for them, and re-layouts  3.04 us

profile of v1, /device:TPU:0, one launch (start us, length us, event | category | flops | bytes accessed | tf_op | source)
XLA Modules:
  0.0 103.6 jit_solution(17628045083015262537)
XLA Ops:
  0.0 0.0 copy-start
  0.0 0.7 copy-done
  0.7 0.0 copy-start.1
  0.7 0.7 copy-done.1
  1.3 0.0 copy-start.2
  1.3 0.7 copy-done.2
  2.0 0.0 copy-start.3
  2.0 0.0 copy-start.4
  2.0 0.0 copy-start.5
  2.0 0.0 copy-start.6
  2.0 0.0 copy-start.7
  2.0 46.4 %plan_and_share.1 = (s32[24,128]{1,0:T(8,128)S(1)}, s32[1]{0:T(128)}, bf16[2,1024,128]{2,1,0:T(8,128)(2,1)S(1)}, bf16[2,1024,128]{2,1,0:T(8,128)(2,1)S(1)}, bf16[3,2,22,8,640]{4,3,2,1,0:T(8,128)(2,1)S(1)}) custom-call(s32[16]{0:T(128)S(1)} %copy-done, s32[8]{0:T(128)S(1)} %copy-done.1, s32[8]{0:T(128)S(1)} %copy-done.2, bf16[64,8,1280]{2,1,0:T(8,128)(2,1)} %bitcast.9, ...), custom_call_target="tpu_custom_call" | custom-call | tf_op jit(solution)/shard_map/plan_and_share/pallas_call | solution.py:961
  49.0 0.0 copy-done.3
  49.1 0.0 copy-done.4
  49.1 0.0 copy-done.5
  49.1 0.0 copy-done.6
  49.1 0.0 copy-done.7
  49.1 53.4 %conditional.1 = (bf16[8,16,5120]{2,1,0:T(8,128)(2,1)S(1)}) conditional(s32[]{:T(128)} %bitcast.8, (s32[24,128]{1,0:T(8,128)S(1)}, bf16[64,8,1280]{2,1,0:T(8,128)(2,1)S(1)}, bf16[2,1024,256]{2,1,0:T(8,128)(2,1)S(1)}, bf16[2,1024,256]{2,1,0:T(8,128)(2,1)S(1)}, bf16[2,1024,128]{2,1,0:T(8,128)(2,1)S(1)}, ...), branch_computations={%region_0.0_spmd, %region_1.0_spmd, %region_2.0_spmd, %region_3.0_... | conditional | bytes 8 | solution.py:1017
  49.1 53.1 %packed_prefix_attention_1.1 = bf16[16,8,5120]{2,1,0:T(8,128)(2,1)S(1)} custom-call(s32[24,128]{1,0:T(8,128)S(1)} %get-tuple-element.149.tables, bf16[64,8,1280]{2,1,0:T(8,128)(2,1)S(1)} %get-tuple-element.150.q_ref, bf16[2,1024,256]{2,1,0:T(8,128)(2,1)S(1)} %get-tuple-element.151.k_ref, bf16[2,1024,256]{2,1,0:T(8,128)(2,1)S(1)} %get-tuple-element.152.v_ref, ...), custom_call_target="tpu_custom_call" | custom-call | tf_op jit(solution)/shard_map/cond/branch_1_fun/packed_prefix_attention_1/pallas_call | solution.py:991
  102.5 1.1 %copy.24 = bf16[8,16,5120]{2,1,0:T(8,128)(2,1)} copy(bf16[8,16,5120]{2,1,0:T(8,128)(2,1)S(1)} %get-tuple-element.213) | data formatting | bytes 2621440
Async XLA Ops:
  0.0 0.7 copy-start
  0.7 0.7 copy-start.1
  1.3 0.7 copy-start.2
  2.0 47.1 %copy-start.3 = (bf16[8,64,1280]{2,1,0:T(8,128)(2,1)S(1)}, bf16[8,64,1280]{2,1,0:T(8,128)(2,1)}, u32[]{:S(2)}) copy-start(bf16[8,64,1280]{2,1,0:T(8,128)(2,1)} %param.15) | copy-start | bytes 3932164
  2.0 47.1 %copy-start.4 = (bf16[2,1024,256]{2,1,0:T(8,128)(2,1)S(1)}, bf16[2,1024,256]{2,1,0:T(8,128)(2,1)}, u32[]{:S(2)}) copy-start(bf16[2,1024,256]{2,1,0:T(8,128)(2,1)} %k_ref.1) | copy-start | bytes 3145732
  2.0 47.1 %copy-start.5 = (bf16[2,1024,256]{2,1,0:T(8,128)(2,1)S(1)}, bf16[2,1024,256]{2,1,0:T(8,128)(2,1)}, u32[]{:S(2)}) copy-start(bf16[2,1024,256]{2,1,0:T(8,128)(2,1)} %v_ref.1) | copy-start | bytes 3145732
  2.0 47.1 %copy-start.6 = (f32[8,8,128]{2,1,0:T(8,128)S(1)}, f32[8,8,128]{2,1,0:T(8,128)}, u32[]{:S(2)}) copy-start(f32[8,8,128]{2,1,0:T(8,128)} %constant.11.clone.sin_ref) | copy-start | bytes 98308
  2.0 47.1 %copy-start.7 = (f32[8,8,128]{2,1,0:T(8,128)S(1)}, f32[8,8,128]{2,1,0:T(8,128)}, u32[]{:S(2)}) copy-start(f32[8,8,128]{2,1,0:T(8,128)} %constant.10.clone.cos_ref) | copy-start | bytes 98308
